TPU v7x, 128 devices: a whole 4x4x4 slice. The times are simulated.
128 devices in a mesh: grp: 4 (over z_lo, core), tile: 32 (over x, z_hi, y).
Axes of the slice: x: 4, y: 4, z: 4 (z_hi: 2, z_lo: 2; z = z_hi * 2 + z_lo), core: 2. Of those that a mesh axis runs over, the one named last changes fastest.
Arguments:
- amplitudes: bfloat16 [160, 4, 983040], P(None, None, ('grp', 'tile')), may hold values from -6 to 6
- w_vvvo: bfloat16 [1024, 983040], P(None, ('grp', 'tile')), may hold values from -0.0234375 to 0.0234375
- pair_mask: int32 [4096], P(('grp', 'tile')), may hold values from 0 to 1, as said below
- owner_map: int32 [32], replicated, may hold values from 0 to 31, each once
Outputs:
- sigma_one: float32 [160, 4, 1024], P('tile', None, 'grp')
Inputs may be any that keep to these rules, and one draw needn't show every extreme that they name: `pair_mask`: in each aligned block of 32 pairs at most 24 are 1 and at least one is; some block has exactly 24 and some block exactly one. `owner_map`: a permutation of the row blocks.
All inputs are finite; a program needn't handle non-finite values.
Results may differ from a plain program's by a relative error of at most 0.0003.
Values sent between devices are 32-bit elements; how exact they have to be, the bound alone decides.
No kernel may reach another device: no remote copies, remote signals or barrier semaphores. Data moves between devices by JAX's collectives and lax.ppermute only.
A program may use at most 128 MiB of HBM per device.

v0:
```python
import jax
import jax.numpy as jnp
from jax import lax
from jax.sharding import PartitionSpec as P


def split_up(shard, dim, size):
    before, after = (shard.shape[:dim], shard.shape[dim + 1 :])
    return jnp.moveaxis(shard.reshape(*before, size, -1, *after), dim, 0)


def sent_and_summed(shard, axis, dim):
    parts = split_up(shard, dim, lax.axis_size(axis))
    arrived = lax.all_to_all(parts, axis, split_axis=0, concat_axis=0, tiled=True)
    return arrived.sum(axis=0)


def full_product(amp_flat, weights, mask_cols):
    masked = amp_flat * mask_cols
    return lax.dot_general(
        weights, masked, (((1,), (1,)), ((), ())), preferred_element_type=jnp.float32
    )


def shards(amplitudes, w_vvvo, pair_mask, owner_map):
    occ_total, root_count, pair_cols = amplitudes.shape
    virt_total = w_vvvo.shape[0]
    tile_count = lax.axis_size("tile")
    occ_rows = occ_total // tile_count
    pair_count = pair_mask.shape[0]
    occ_width = pair_cols // pair_count
    mask_cols = jnp.repeat(pair_mask.astype(jnp.bfloat16), occ_width, total_repeat_length=pair_cols)
    virt_rows = virt_total // lax.axis_size("grp")
    amp_flat = amplitudes.reshape(occ_total * root_count, pair_cols)
    term = full_product(amp_flat, w_vvvo, mask_cols)
    term = term.reshape(virt_rows * lax.axis_size("grp"), tile_count, occ_rows * root_count)
    owned = sent_and_summed(
        jnp.take(term, owner_map, axis=1).reshape(
            virt_rows * lax.axis_size("grp"), occ_total * root_count
        ),
        "grp",
        0,
    )
    partial_value = sent_and_summed(owned, "tile", 1)
    sigma_one = jnp.transpose(partial_value.reshape(virt_rows, occ_rows, root_count), (1, 2, 0))
    return sigma_one


def solution(mesh):
    return jax.shard_map(
        shards,
        mesh=mesh,
        in_specs=(
            P(None, None, ("grp", "tile")),
            P(None, ("grp", "tile")),
            P(("grp", "tile")),
            P(),
        ),
        out_specs=P("tile", None, "grp"),
        check_vma=False,
    )
```

profile of v0, /device:TPU:0, one launch (start us, length us, event | category | flops | bytes accessed | tf_op | source)
XLA Modules:
  0.0 125.7 jit_solution(4318091118811727333)
XLA Ops:
  0.0 0.7 convert_element_type.3
  0.7 0.7 fusion.6
  1.4 0.7 fusion.7
  2.1 0.7 compare_select_fusion
  2.7 0.7 compare_and_fusion
  3.4 0.0 copy-start.2
  3.4 0.0 copy-start.3
  3.4 0.0 copy-start.4
  3.4 0.0 copy-start.5
  3.5 0.0 copy-start.6
  3.5 0.0 copy-start.7
  3.5 0.0 copy-start.8
  3.5 0.0 copy-start.9
  3.5 0.0 copy-start.10
  3.5 0.0 copy-start.11
  3.5 0.0 copy-start.12
  3.5 0.0 copy-start.13
  3.6 0.0 copy-start.14
  3.6 0.0 copy-start.15
  3.6 0.0 copy-start.16
  3.6 0.0 copy-start.17
  3.6 0.0 copy-start.18
  3.6 0.0 copy-start.19
  3.6 0.0 copy-start.20
  3.6 0.0 copy-start.21
  3.7 0.0 copy-start.22
  3.7 0.0 copy-start.23
  3.7 0.0 copy-start.24
  3.7 0.0 copy-start.25
  3.7 0.0 copy-start.26
  3.7 0.0 copy-start.27
  3.7 0.0 copy-start.28
  3.8 0.0 copy-start.29
  3.8 0.0 copy-start.30
  3.8 13.3 %reshape.107 = bf16[640,7680]{1,0:T(8,128)(2,1)} reshape(bf16[160,4,7680]{2,1,0:T(4,128)(2,1)} %param.6) | data formatting | bytes 19660800 | tf_op jit(solution)/shard_map/reshape | solution.py:34
  17.1 0.0 copy-done
  17.1 0.0 copy-done.1
  17.1 0.0 copy-done.2
  17.1 0.0 copy-done.3
  17.1 0.0 copy-done.4
  17.1 0.0 copy-done.5
  17.2 0.0 copy-done.6
  17.2 0.0 copy-done.7
  17.2 0.0 copy-done.8
  17.2 0.0 copy-done.9
  17.2 0.0 copy-done.10
  17.2 0.0 copy-done.11
  17.2 0.0 copy-done.12
  17.2 0.0 copy-done.13
  17.4 19.7 %select_select_fusion = bf16[7680]{0:T(1024)(128)(2,1)S(1)} fusion(pred[7680]{0:T(1024)(128)(4,1)S(1)} %copy-done, pred[7680]{0:T(1024)(128)(4,1)S(1)} %copy-done.1, pred[7680]{0:T(1024)(128)(4,1)S(1)} %copy-done.2, pred[7680]{0:T(1024)(128)(4,1)S(1)} %copy-done.3, pred[7680]{0:T(1024)(128)(4,1)S(1)} %copy-done.4, pred[7680]{0:T(1024)(128)(4,1)S(1)} %copy-done.5, ...), kind=kLoop, calls=%fused_computation.6 | loop fusion | flops 238080 | bytes 253504 | tf_op jit(solution)/shard_map/jit(_take)/gather | solution.py:32
  37.1 16.8 %fusion.3 = f32[1024,640]{0,1:T(8,128)} fusion(bf16[1024,7680]{1,0:T(8,128)(2,1)} %param.7, bf16[640,7680]{1,0:T(8,128)(2,1)} %reshape.107, bf16[7680]{0:T(1024)(128)(2,1)S(1)} %select_select_fusion), kind=kOutput, calls=%fused_computation.4 | convolution fusion | flops 10071244800 | bytes 28195840 | tf_op jit(solution)/shard_map/dot_general | solution.py:20
  53.9 2.5 %reshape.108 = f32[1024,32,20]{0,2,1:T(8,128)S(1)} reshape(f32[1024,640]{0,1:T(8,128)} %fusion.3) | data formatting | bytes 5242880 | tf_op jit(solution)/shard_map/reshape | solution.py:36
  56.4 2.4 %gather_fusion = f32[32,1024,20]{1,2,0:T(8,128)} fusion(f32[1024,32,20]{0,2,1:T(8,128)S(1)} %reshape.108, s32[1024]{0:T(1024)S(1)} %pad_clamp_fusion), kind=kCustom, calls=%fused_computation | custom fusion | bytes 5243008 | tf_op jit(solution)/shard_map/jit(_take)/gather | solution.py:38
  58.8 3.2 %gather.12 = f32[4,256,640]{1,0,2:T(4,128)S(1)} reshape(f32[1024,32,20]{0,2,1:T(8,128)} %bitcast.46) | data formatting | bytes 5242880 | tf_op jit(solution)/shard_map/jit(_take)/gather | solution.py:38
  62.0 0.1 broadcast_in_dim.25
  62.1 0.1 broadcast_in_dim.26
  62.2 2.3 %broadcast_select_fusion = f32[4,256,640]{1,0,2:T(4,128)S(1)} fusion(f32[4,256,640]{1,0,2:T(4,128)S(1)} %gather.12, pred[640]{0:T(1024)(128)(4,1)S(1)} %broadcast_in_dim.26), kind=kLoop, calls=%fused_computation.5 | loop fusion | flops 655360 | bytes 5243520 | tf_op jit(solution)/shard_map/jit(_take)/select_n | solution.py:38
  64.5 0.5 copy.5
  65.0 34.4 %all_to_all.10 = f32[4,256,640]{1,2,0:T(8,128)S(1)} all-to-all(f32[4,256,640]{1,2,0:T(8,128)S(1)} %copy.5), channel_id=1, replica_groups=mesh['grp'=4,'tile'=32] {'grp'}, dimensions={0} | all-to-all | bytes 5242880 | tf_op jit(solution)/shard_map/all_to_all | solution.py:14
  99.4 0.2 reduce_sum.18
  99.7 0.1 reshape.109
  99.7 25.3 %all_to_all.11 = f32[32,256,20]{1,2,0:T(8,128)S(1)} all-to-all(f32[32,256,20]{1,2,0:T(8,128)S(1)} %bitcast.47), channel_id=1, replica_groups=mesh['grp'=4,'tile'=32] {'tile'}, dimensions={0} | all-to-all | bytes 1310720 | tf_op jit(solution)/shard_map/all_to_all | solution.py:14
  125.0 0.1 reduce_sum.19
  125.1 0.6 reshape.110
  (20 shorter events, 0.0 us)
Async XLA Ops:
  3.4 13.7 %copy-start = (pred[7680]{0:T(1024)(128)(4,1)S(1)}, pred[7680]{0:T(1024)(128)(4,1)}, u32[]{:S(2)}) copy-start(pred[7680]{0:T(1024)(128)(4,1)} %constant.152) | copy-start | bytes 23044
  3.4 13.7 %copy-start.1 = (pred[7680]{0:T(1024)(128)(4,1)S(1)}, pred[7680]{0:T(1024)(128)(4,1)}, u32[]{:S(2)}) copy-start(pred[7680]{0:T(1024)(128)(4,1)} %constant.153) | copy-start | bytes 23044
  3.4 13.7 %copy-start.2 = (pred[7680]{0:T(1024)(128)(4,1)S(1)}, pred[7680]{0:T(1024)(128)(4,1)}, u32[]{:S(2)}) copy-start(pred[7680]{0:T(1024)(128)(4,1)} %constant.154) | copy-start | bytes 23044
  3.4 13.7 %copy-start.3 = (pred[7680]{0:T(1024)(128)(4,1)S(1)}, pred[7680]{0:T(1024)(128)(4,1)}, u32[]{:S(2)}) copy-start(pred[7680]{0:T(1024)(128)(4,1)} %constant.155) | copy-start | bytes 23044
  3.4 13.7 %copy-start.4 = (pred[7680]{0:T(1024)(128)(4,1)S(1)}, pred[7680]{0:T(1024)(128)(4,1)}, u32[]{:S(2)}) copy-start(pred[7680]{0:T(1024)(128)(4,1)} %constant.156) | copy-start | bytes 23044
  3.4 13.7 %copy-start.5 = (pred[7680]{0:T(1024)(128)(4,1)S(1)}, pred[7680]{0:T(1024)(128)(4,1)}, u32[]{:S(2)}) copy-start(pred[7680]{0:T(1024)(128)(4,1)} %constant.157) | copy-start | bytes 23044
  3.5 13.7 %copy-start.6 = (pred[7680]{0:T(1024)(128)(4,1)S(1)}, pred[7680]{0:T(1024)(128)(4,1)}, u32[]{:S(2)}) copy-start(pred[7680]{0:T(1024)(128)(4,1)} %constant.158) | copy-start | bytes 23044
  3.5 13.7 %copy-start.7 = (pred[7680]{0:T(1024)(128)(4,1)S(1)}, pred[7680]{0:T(1024)(128)(4,1)}, u32[]{:S(2)}) copy-start(pred[7680]{0:T(1024)(128)(4,1)} %constant.159) | copy-start | bytes 23044
  3.5 13.7 %copy-start.8 = (pred[7680]{0:T(1024)(128)(4,1)S(1)}, pred[7680]{0:T(1024)(128)(4,1)}, u32[]{:S(2)}) copy-start(pred[7680]{0:T(1024)(128)(4,1)} %constant.160) | copy-start | bytes 23044
  3.5 13.7 %copy-start.9 = (pred[7680]{0:T(1024)(128)(4,1)S(1)}, pred[7680]{0:T(1024)(128)(4,1)}, u32[]{:S(2)}) copy-start(pred[7680]{0:T(1024)(128)(4,1)} %constant.161) | copy-start | bytes 23044
  3.5 13.7 %copy-start.10 = (pred[7680]{0:T(1024)(128)(4,1)S(1)}, pred[7680]{0:T(1024)(128)(4,1)}, u32[]{:S(2)}) copy-start(pred[7680]{0:T(1024)(128)(4,1)} %constant.162) | copy-start | bytes 23044
  3.5 13.7 %copy-start.11 = (pred[7680]{0:T(1024)(128)(4,1)S(1)}, pred[7680]{0:T(1024)(128)(4,1)}, u32[]{:S(2)}) copy-start(pred[7680]{0:T(1024)(128)(4,1)} %constant.163) | copy-start | bytes 23044
  3.5 13.7 %copy-start.12 = (pred[7680]{0:T(1024)(128)(4,1)S(1)}, pred[7680]{0:T(1024)(128)(4,1)}, u32[]{:S(2)}) copy-start(pred[7680]{0:T(1024)(128)(4,1)} %constant.164) | copy-start | bytes 23044
  3.5 13.7 %copy-start.13 = (pred[7680]{0:T(1024)(128)(4,1)S(1)}, pred[7680]{0:T(1024)(128)(4,1)}, u32[]{:S(2)}) copy-start(pred[7680]{0:T(1024)(128)(4,1)} %constant.165) | copy-start | bytes 23044
  3.6 13.7 %copy-start.14 = (pred[7680]{0:T(1024)(128)(4,1)S(1)}, pred[7680]{0:T(1024)(128)(4,1)}, u32[]{:S(2)}) copy-start(pred[7680]{0:T(1024)(128)(4,1)} %constant.166) | copy-start | bytes 23044
  3.6 13.7 %copy-start.15 = (pred[7680]{0:T(1024)(128)(4,1)S(1)}, pred[7680]{0:T(1024)(128)(4,1)}, u32[]{:S(2)}) copy-start(pred[7680]{0:T(1024)(128)(4,1)} %constant.167) | copy-start | bytes 23044
  3.6 13.7 %copy-start.16 = (pred[7680]{0:T(1024)(128)(4,1)S(1)}, pred[7680]{0:T(1024)(128)(4,1)}, u32[]{:S(2)}) copy-start(pred[7680]{0:T(1024)(128)(4,1)} %constant.168) | copy-start | bytes 23044
  3.6 13.7 %copy-start.17 = (pred[7680]{0:T(1024)(128)(4,1)S(1)}, pred[7680]{0:T(1024)(128)(4,1)}, u32[]{:S(2)}) copy-start(pred[7680]{0:T(1024)(128)(4,1)} %constant.169) | copy-start | bytes 23044
  3.6 13.7 %copy-start.18 = (pred[7680]{0:T(1024)(128)(4,1)S(1)}, pred[7680]{0:T(1024)(128)(4,1)}, u32[]{:S(2)}) copy-start(pred[7680]{0:T(1024)(128)(4,1)} %constant.170) | copy-start | bytes 23044
  3.6 13.7 %copy-start.19 = (pred[7680]{0:T(1024)(128)(4,1)S(1)}, pred[7680]{0:T(1024)(128)(4,1)}, u32[]{:S(2)}) copy-start(pred[7680]{0:T(1024)(128)(4,1)} %constant.171) | copy-start | bytes 23044
  3.6 13.7 %copy-start.20 = (pred[7680]{0:T(1024)(128)(4,1)S(1)}, pred[7680]{0:T(1024)(128)(4,1)}, u32[]{:S(2)}) copy-start(pred[7680]{0:T(1024)(128)(4,1)} %constant.172) | copy-start | bytes 23044
  3.6 13.7 %copy-start.21 = (pred[7680]{0:T(1024)(128)(4,1)S(1)}, pred[7680]{0:T(1024)(128)(4,1)}, u32[]{:S(2)}) copy-start(pred[7680]{0:T(1024)(128)(4,1)} %constant.173) | copy-start | bytes 23044
  3.7 13.7 %copy-start.22 = (pred[7680]{0:T(1024)(128)(4,1)S(1)}, pred[7680]{0:T(1024)(128)(4,1)}, u32[]{:S(2)}) copy-start(pred[7680]{0:T(1024)(128)(4,1)} %constant.174) | copy-start | bytes 23044
  3.7 13.7 %copy-start.23 = (pred[7680]{0:T(1024)(128)(4,1)S(1)}, pred[7680]{0:T(1024)(128)(4,1)}, u32[]{:S(2)}) copy-start(pred[7680]{0:T(1024)(128)(4,1)} %constant.175) | copy-start | bytes 23044
  3.7 13.7 %copy-start.24 = (pred[7680]{0:T(1024)(128)(4,1)S(1)}, pred[7680]{0:T(1024)(128)(4,1)}, u32[]{:S(2)}) copy-start(pred[7680]{0:T(1024)(128)(4,1)} %constant.176) | copy-start | bytes 23044
  3.7 13.6 %copy-start.25 = (pred[7680]{0:T(1024)(128)(4,1)S(1)}, pred[7680]{0:T(1024)(128)(4,1)}, u32[]{:S(2)}) copy-start(pred[7680]{0:T(1024)(128)(4,1)} %constant.177) | copy-start | bytes 23044
  3.7 13.6 %copy-start.26 = (pred[7680]{0:T(1024)(128)(4,1)S(1)}, pred[7680]{0:T(1024)(128)(4,1)}, u32[]{:S(2)}) copy-start(pred[7680]{0:T(1024)(128)(4,1)} %constant.178) | copy-start | bytes 23044
  3.7 13.6 %copy-start.27 = (pred[7680]{0:T(1024)(128)(4,1)S(1)}, pred[7680]{0:T(1024)(128)(4,1)}, u32[]{:S(2)}) copy-start(pred[7680]{0:T(1024)(128)(4,1)} %constant.179) | copy-start | bytes 23044
  3.7 13.6 %copy-start.28 = (pred[7680]{0:T(1024)(128)(4,1)S(1)}, pred[7680]{0:T(1024)(128)(4,1)}, u32[]{:S(2)}) copy-start(pred[7680]{0:T(1024)(128)(4,1)} %constant.180) | copy-start | bytes 23044
  3.8 13.6 %copy-start.29 = (pred[7680]{0:T(1024)(128)(4,1)S(1)}, pred[7680]{0:T(1024)(128)(4,1)}, u32[]{:S(2)}) copy-start(pred[7680]{0:T(1024)(128)(4,1)} %constant.181) | copy-start | bytes 23044
  3.8 13.6 %copy-start.30 = (pred[7680]{0:T(1024)(128)(4,1)S(1)}, pred[7680]{0:T(1024)(128)(4,1)}, u32[]{:S(2)}) copy-start(pred[7680]{0:T(1024)(128)(4,1)} %constant.182) | copy-start | bytes 23044
where the time goes:
time: 127 us; the launch traced here: 126 us
  blocking collectives  59.6 us (47%)
  local copies, waits for them, and re-layouts  24.5 us (19%)
  other arithmetic  24.3 us (19%)
  matrix products  16.8 us (13%)
    all_to_all x2, blocking collectives, sent_and_summed(): lax.all_to_all(parts, axis, split_axis=0, concat_axis=0, tiled=True)  59.6 us
    gather x1, other arithmetic, shards(): jnp.repeat(pair_mask.astype(jnp.bfloat16), occ_width, total_repeat_length...  19.7 us
    dot_general x1, matrix products, full_product(): lax.dot_general(weights, masked, (((1,), (1,)), ((), ())), preferred_elem...  16.8 us
    reshape x1, local copies, waits for them, and re-layouts, shards(): amp_flat = amplitudes.reshape(occ_total * root_count, pair_cols)  13.3 us
    gather x2, local copies, waits for them, and re-layouts, shards(): jnp.take(term, owner_map, axis=1)  5.6 us
    select_n x2, other arithmetic, shards(): jnp.take(term, owner_map, axis=1)  2.97 us

commit v1 on v0

v1 whole, which is shorter than its diff:
```python
import functools

import jax
import jax.numpy as jnp
from jax import lax
from jax.experimental import pallas as pl
from jax.experimental.pallas import tpu as pltpu
from jax.sharding import PartitionSpec as P

AXES = ("grp", "tile")
TORUS = 4
ROWS = 20
UNIT = 2 * ROWS
HALF = 512
VIRT = 256
NT = (((1,), (1,)), ((), ()))
BOUNDS = (0, 512, 1280, 2560, 4608, 7680)
DEPTH = 3


def coords(i):
    g, t = divmod(i, 32)
    z_lo, core = divmod(g, 2)
    x, r = divmod(t, 8)
    z_hi, y = divmod(r, 4)
    return x, y, z_hi * 2 + z_lo, core


def index(x, y, z, core):
    return ((z % 2) * 2 + core) * 32 + x * 8 + (z // 2) * 4 + y


def pairs(move):
    return [(i, index(*move(*coords(i)))) for i in range(128)]


OTHER_CORE = pairs(lambda x, y, z, c: (x, y, z, 1 - c))


def along_own(k):
    return pairs(lambda x, y, z, c: (x, y ^ k, z, c) if c else (x ^ k, y, z, c))


def plane_groups():
    groups = {}
    for i in range(128):
        x, y, z, c = coords(i)
        key, place = ((c, y), (x, z)) if c else ((c, x), (y, z))
        groups.setdefault(key, []).append((place, i))
    return [[i for _, i in sorted(g)] for g in groups.values()]


def mask_row(mask_ref, c0, width, occ):
    col = lax.broadcasted_iota(jnp.int32, (1, width), 1) + c0
    row = jnp.zeros((1, width), jnp.float32)
    for p in range(c0 // occ, (c0 + width - 1) // occ + 1):
        inside = (col >= p * occ) & (col < (p + 1) * occ)
        row = jnp.where(inside, mask_ref[p].astype(jnp.float32), row)
    return row.astype(jnp.bfloat16)


def here():
    g, t = lax.axis_index("grp"), lax.axis_index("tile")
    return lax.rem(g, 2), t // 8, lax.rem(t, 4)


def put(out_ref, total, side, x_here, y_here):
    for x in range(TORUS):
        for y in range(TORUS):
            u = x * TORUS + y
            slot = jnp.where(side == 0, (x ^ x_here) * TORUS + y, (y ^ y_here) * TORUS + x)
            out_ref[slot] = total[u * UNIT : (u + 1) * UNIT]


def columns(k):
    return pl.ds(BOUNDS[k], BOUNDS[k + 1] - BOUNDS[k])


def start_weights(w_ref, w_s, w_sem, side, k):
    for z_lo in range(2):
        pltpu.make_async_copy(
            w_ref.at[z_lo, side, :, columns(k)],
            w_s.at[pl.ds(z_lo * VIRT, VIRT), columns(k)],
            w_sem.at[k],
        ).start()


def wait_for(ref, sem):
    pltpu.make_async_copy(ref, ref, sem).wait()


def first_half(
    occ, owner_hbm, mask_hbm, amp_ref, w_ref, out_ref, x_ref,
    owner_ref, mask_ref, a_s, w_s, acc, a_sem, w_sem, s_sem,
):
    core, x_here, y_here = here()
    side = 1 - core
    blocks = len(BOUNDS) - 1
    rows = a_s.shape[0] // 32
    tables = [
        pltpu.make_async_copy(owner_hbm, owner_ref, s_sem.at[0]),
        pltpu.make_async_copy(mask_hbm, mask_ref, s_sem.at[1]),
    ]
    for table in tables:
        table.start()

    def start_amplitudes(k):
        for x in range(TORUS):
            for y in range(TORUS):
                for z_hi in range(2):
                    source = owner_ref[x * 8 + z_hi * 4 + y]
                    place = (x * TORUS + y) * 2 + z_hi
                    pltpu.make_async_copy(
                        amp_ref.at[pl.ds(source * rows, rows), :, columns(k)],
                        a_s.at[pl.ds(place * rows, rows), :, columns(k)],
                        a_sem.at[k],
                    ).start()

    for k in range(DEPTH):
        start_weights(w_ref, w_s, w_sem, side, k)
    for table in tables:
        table.wait()
    for k in range(DEPTH):
        start_amplitudes(k)
    for k in range(blocks):
        if k + DEPTH < blocks:
            start_weights(w_ref, w_s, w_sem, side, k + DEPTH)
            start_amplitudes(k + DEPTH)
        c0, c1 = BOUNDS[k], BOUNDS[k + 1]
        wait_for(a_s.at[:, :, columns(k)], a_sem.at[k])
        amp = a_s[:, :, c0:c1].reshape(x_ref.shape[0], c1 - c0)
        x_ref[:, c0:c1] = amp * mask_row(mask_ref, c0, c1 - c0, occ)
        wait_for(w_s.at[:, columns(k)], w_sem.at[k])
        part = lax.dot_general(x_ref[:, c0:c1], w_s[:, c0:c1], NT, preferred_element_type=jnp.float32)
        if k == 0:
            acc[...] = part
        elif k < blocks - 1:
            acc[...] += part
        else:
            put(out_ref, acc[...] + part, side, x_here, y_here)


def second_half(x_ref, w_ref, out_ref, w_s, acc, w_sem):
    side, x_here, y_here = here()
    blocks = len(BOUNDS) - 1
    for k in range(DEPTH):
        start_weights(w_ref, w_s, w_sem, side, k)
    for k in range(blocks):
        if k + DEPTH < blocks:
            start_weights(w_ref, w_s, w_sem, side, k + DEPTH)
        c0, c1 = BOUNDS[k], BOUNDS[k + 1]
        wait_for(w_s.at[:, columns(k)], w_sem.at[k])
        part = lax.dot_general(x_ref[:, c0:c1], w_s[:, c0:c1], NT, preferred_element_type=jnp.float32)
        if k == 0:
            acc[...] = part
        elif k < blocks - 1:
            acc[...] += part
        else:
            put(out_ref, acc[...] + part, side, x_here, y_here)


def shards(amplitudes, w_vvvo, pair_mask, owner_map):
    occ_total, roots, cols = amplitudes.shape
    rows = occ_total * roots
    w4 = w_vvvo.reshape(2, 2, VIRT, cols)
    any_spec = pl.BlockSpec(memory_space=pl.ANY)
    hbm = pl.BlockSpec(memory_space=pltpu.HBM)
    vmem = pl.BlockSpec(memory_space=pltpu.VMEM)
    part_shape = pltpu.VMEM((TORUS * TORUS, UNIT, HALF), jnp.float32)
    blocks = len(BOUNDS) - 1
    params = pltpu.CompilerParams(vmem_limit_bytes=40 * 2**20)
    flops = 2 * rows * HALF * cols
    theirs, masked = pl.pallas_call(
        functools.partial(first_half, cols // pair_mask.shape[0]),
        in_specs=[any_spec, any_spec, hbm, hbm],
        out_specs=[vmem, vmem],
        out_shape=[part_shape, pltpu.VMEM((rows, cols), jnp.bfloat16)],
        scratch_shapes=[
            pltpu.SMEM(owner_map.shape, jnp.int32),
            pltpu.SMEM(pair_mask.shape, jnp.int32),
            pltpu.VMEM(amplitudes.shape, jnp.bfloat16),
            pltpu.VMEM((HALF, cols), jnp.bfloat16),
            pltpu.VMEM((rows, HALF), jnp.float32),
            pltpu.SemaphoreType.DMA((blocks,)),
            pltpu.SemaphoreType.DMA((blocks,)),
            pltpu.SemaphoreType.DMA((2,)),
        ],
        compiler_params=params,
        cost_estimate=pl.CostEstimate(flops=flops, bytes_accessed=18 * 10**6, transcendentals=0),
        name="their_half",
    )(owner_map, pair_mask, amplitudes, w4)
    from_core = lax.ppermute(theirs, AXES, OTHER_CORE)
    own = pl.pallas_call(
        second_half,
        in_specs=[vmem, hbm],
        out_specs=vmem,
        out_shape=part_shape,
        scratch_shapes=[
            pltpu.VMEM((HALF, cols), jnp.bfloat16),
            pltpu.VMEM((rows, HALF), jnp.float32),
            pltpu.SemaphoreType.DMA((blocks,)),
        ],
        compiler_params=params,
        cost_estimate=pl.CostEstimate(flops=flops, bytes_accessed=8 * 10**6, transcendentals=0),
        name="own_half",
    )(masked, w4)
    chip = (own + from_core).reshape(TORUS, TORUS, UNIT, HALF)
    arrived = [lax.ppermute(chip[k], AXES, along_own(k)) for k in (2, 1, 3)]
    plane = chip[0] + arrived[0] + arrived[1] + arrived[2]
    sent = plane.reshape(TORUS, 2, ROWS, 2, VIRT).transpose(0, 1, 3, 2, 4).reshape(16, ROWS, VIRT)
    got = lax.all_to_all(sent, AXES, 0, 0, axis_index_groups=plane_groups(), tiled=True)
    return got.sum(axis=0).reshape(ROWS // roots, roots, VIRT)


def solution(mesh):
    return jax.shard_map(
        shards,
        mesh=mesh,
        in_specs=(P(None, None, AXES), P(None, AXES), P(AXES), P()),
        out_specs=P("tile", None, "grp"),
        check_vma=False,
    )
```

time: 127 us -> 47.8 us (0.38)
  blocking collectives: 59.6 us -> 17 us
  other arithmetic: 24.3 us -> 0.43 us
  local copies, waits for them, and re-layouts: 24.5 us -> 2.24 us
  matrix products: 16.8 us -> 0 us
  Pallas kernels: 0 us -> 15.4 us
  waiting for transfers between devices: 0 us -> 8.06 us
  starting transfers between devices: 0 us -> 4.44 us
    all_to_all x2 -> x1, blocking collectives: 59.6 us -> 17 us  [shards(): lax.all_to_all(sent, AXES, 0, 0, axis_index_groups=plane_groups(), tiled=...]
    gather x2 -> x0, other arithmetic: 19.7 us -> none  [the longest x1 19.7 us: shards(): jnp.repeat(pair_mask.astype(jnp.bfloat16), occ_width, total_repeat_length...]
    dot_general x1 -> x0, matrix products: 16.8 us -> none  [full_product(): lax.dot_general(weights, masked, (((1,), (1,)), ((), ())), preferred_elem...]
    reshape x4 -> x3, local copies, waits for them, and re-layouts: 16.6 us -> 0.86 us  [the longest x1 0.62 us: shards(): return got.sum(axis=0).reshape(ROWS // roots, roots, VIRT)]
    pallas_call x0 -> x2, Pallas kernels: none -> 15.4 us  [the longest x1 8.72 us: shards(): pl.pallas_call(functools.partial(first_half, cols // pair_mask.shape[0]),...]
    ppermute x0 -> x4, waiting for transfers between devices: none -> 8.06 us  [the longest x3 8.05 us: shards(): arrived = [lax.ppermute(chip[k], AXES, along_own(k)) for k in (2, 1, 3)]]
    gather x4 -> x0, local copies, waits for them, and re-layouts: 7.02 us -> none  [the longest x2 5.6 us: shards(): jnp.take(term, owner_map, axis=1)]
    ppermute x0 -> x4, starting transfers between devices: none -> 4.44 us  [the longest x3 4.35 us: shards(): arrived = [lax.ppermute(chip[k], AXES, along_own(k)) for k in (2, 1, 3)]]
  transfers between devices with their start and end apart: 0 -> 4, of which waited for: 0 -> 3; matrix products, arithmetic and copies ran while one was open for 0% -> 0% of each run, Pallas kernels for 0% -> 14%
where the time goes in v1:
time: 47.8 us; the launch traced here: 47.6 us
  blocking collectives  17 us (36%)
  Pallas kernels  15.4 us (32%)
  waiting for transfers between devices  8.06 us (17%)
  starting transfers between devices  4.44 us (9%)
  local copies, waits for them, and re-layouts  2.24 us (5%)
    all_to_all x1, blocking collectives, shards(): lax.all_to_all(sent, AXES, 0, 0, axis_index_groups=plane_groups(), tiled=...  17 us
    pallas_call x1, Pallas kernels, shards(): pl.pallas_call(functools.partial(first_half, cols // pair_mask.shape[0]),...  8.72 us
    ppermute x3, waiting for transfers between devices, shards(): arrived = [lax.ppermute(chip[k], AXES, along_own(k)) for k in (2, 1, 3)]  8.05 us
    pallas_call x1, Pallas kernels, shards(): pl.pallas_call(second_half, in_specs=[vmem, hbm], out_specs=vmem, out_sha...  6.67 us
    ppermute x3, starting transfers between devices, shards(): arrived = [lax.ppermute(chip[k], AXES, along_own(k)) for k in (2, 1, 3)]  4.35 us
    unnamed x4, local copies, waits for them, and re-layouts  1.31 us
  transfers between devices with their start and end apart: 4, of which 3 were waited for; matrix products, arithmetic and copies ran while one was open for 0% of the time, Pallas kernels for 14%

profile of v1, /device:TPU:0, one launch (start us, length us, event | category | flops | bytes accessed | tf_op | source)
XLA Modules:
  0.0 47.6 jit_solution(15713573864104877270)
XLA Ops:
  0.0 0.0 copy-start
  0.0 0.7 %copy-done = s32[32]{0:T(128)S(1)} copy-done((s32[32]{0:T(128)S(1)}, s32[32]{0:T(128)}, u32[]{:S(2)}) %copy-start) | copy-done | bytes 152
  0.7 0.0 copy-start.1
  0.7 0.7 %copy-done.1 = s32[32]{0:T(128)S(1)} copy-done((s32[32]{0:T(128)S(1)}, s32[32]{0:T(128)}, u32[]{:S(2)}) %copy-start.1) | copy-done | bytes 152
  1.3 8.7 %their_half.1 = (f32[16,40,512]{2,1,0:T(8,128)S(1)}, bf16[640,7680]{1,0:T(8,128)(2,1)S(1)}) custom-call(s32[32]{0:T(128)S(1)} %copy-done, s32[32]{0:T(128)S(1)} %copy-done.1, bf16[160,4,7680]{2,1,0:T(4,128)(2,1)} %amp_ref.1, bf16[2,2,256,7680]{3,2,1,0:T(8,128)(2,1)} %bitcast.4), custom_call_target="tpu_custom_call" | custom-call | flops 5033164800 | bytes 18000000 | tf_op jit(solution)/shard_map/their_half/pallas_call | solution.py:173
  10.0 0.1 collective-permute-start
  10.1 6.7 %own_half.1 = f32[16,40,512]{2,1,0:T(8,128)S(1)} custom-call(bf16[640,7680]{1,0:T(8,128)(2,1)S(1)} %get-tuple-element.7.x_ref, bf16[2,2,256,7680]{3,2,1,0:T(8,128)(2,1)} %bitcast.5), custom_call_target="tpu_custom_call" | custom-call | flops 5033164800 | bytes 8000000 | tf_op jit(solution)/shard_map/own_half/pallas_call | solution.py:193
  16.8 0.0 collective-permute-done
  16.8 0.3 add.12
  17.1 0.1 fusion.2
  17.2 3.2 %collective-permute-start.1 = (f32[4,40,512]{2,1,0:T(8,128)S(1)}, f32[4,40,512]{2,1,0:T(8,128)S(1)}, u32[]{:S(2)}, u32[]{:S(2)}) collective-permute-start(f32[4,40,512]{2,1,0:T(8,128)S(1)} %get-tuple-element.9), channel_id=1, source_target_pairs={{0,16},{1,17},{2,18},{3,19},{4,20},{5,21},{6,22},{7,23},{8,24},{9,... | collective-permute-start | bytes 983048 | tf_op jit(solution)/shard_map/ppermute | solution.py:208
  20.4 1.1 %collective-permute-start.3 = (f32[4,40,512]{2,1,0:T(8,128)S(1)}, f32[4,40,512]{2,1,0:T(8,128)S(1)}, u32[]{:S(2)}, u32[]{:S(2)}) collective-permute-start(f32[4,40,512]{2,1,0:T(8,128)S(1)} %get-tuple-element.10), channel_id=1, source_target_pairs={{0,24},{1,25},{2,26},{3,27},{4,28},{5,29},{6,30},{7,31},{8,16},{9,... | collective-permute-start | bytes 983048 | tf_op jit(solution)/shard_map/ppermute | solution.py:208
  21.5 0.0 collective-permute-start.2
  21.5 4.4 %collective-permute-done.1 = f32[4,40,512]{2,1,0:T(8,128)S(1)} collective-permute-done((f32[4,40,512]{2,1,0:T(8,128)S(1)}, f32[4,40,512]{2,1,0:T(8,128)S(1)}, u32[]{:S(2)}, u32[]{:S(2)}) %collective-permute-start.1) | collective-permute-done | bytes 327712 | tf_op jit(solution)/shard_map/ppermute | solution.py:208
  25.9 3.4 %collective-permute-done.3 = f32[4,40,512]{2,1,0:T(8,128)S(1)} collective-permute-done((f32[4,40,512]{2,1,0:T(8,128)S(1)}, f32[4,40,512]{2,1,0:T(8,128)S(1)}, u32[]{:S(2)}, u32[]{:S(2)}) %collective-permute-start.3) | collective-permute-done | bytes 327712 | tf_op jit(solution)/shard_map/ppermute | solution.py:208
  29.4 0.2 collective-permute-done.2
  29.6 0.1 fusion.1
  29.7 0.2 reshape.22
  30.0 17.0 %all_to_all.5 = f32[16,20,256]{2,1,0:T(8,128)S(1)} all-to-all(f32[16,20,256]{2,1,0:T(8,128)S(1)} %bitcast.6), channel_id=1, replica_groups={{0,64,4,68,1,65,5,69,2,66,6,70,3,67,7,71},{8,72,12,76,9,73,13,77,10,74,..., dimensions={0} | all-to-all | bytes 655360 | tf_op jit(solution)/shard_map/all_to_all | solution.py:211
  47.0 0.6 %reshape.24 = f32[5,4,256]{2,1,0:T(4,128)} reshape(f32[20,256]{1,0:T(8,128)S(1)} %reduce_sum.9) | data formatting | bytes 40960 | tf_op jit(solution)/shard_map/reshape | solution.py:212
  (2 shorter events, 0.1 us)
Async XLA Ops:
  0.0 0.7 %copy-start = (s32[32]{0:T(128)S(1)}, s32[32]{0:T(128)}, u32[]{:S(2)}) copy-start(s32[32]{0:T(128)} %owner_hbm.1) | copy-start | bytes 388
  0.7 0.7 %copy-start.1 = (s32[32]{0:T(128)S(1)}, s32[32]{0:T(128)}, u32[]{:S(2)}) copy-start(s32[32]{0:T(128)} %mask_hbm.1) | copy-start | bytes 388
  10.0 6.8 %collective-permute-start = (f32[16,40,512]{2,1,0:T(8,128)S(1)}, f32[16,40,512]{2,1,0:T(8,128)S(1)}, u32[]{:S(2)}, u32[]{:S(2)}) collective-permute-start(f32[16,40,512]{2,1,0:T(8,128)S(1)} %get-tuple-element.8), channel_id=1, source_target_pairs={{0,32},{1,33},{2,34},{3,35},{4,36},{5,37},{6,38},{7,39},{8,40},{9,... | collective-permute-start | bytes 3932168 | tf_op jit(solution)/shard_map/ppermute | solution.py:192
  17.2 8.7 %collective-permute-start.1 = (f32[4,40,512]{2,1,0:T(8,128)S(1)}, f32[4,40,512]{2,1,0:T(8,128)S(1)}, u32[]{:S(2)}, u32[]{:S(2)}) collective-permute-start(f32[4,40,512]{2,1,0:T(8,128)S(1)} %get-tuple-element.9), channel_id=1, source_target_pairs={{0,16},{1,17},{2,18},{3,19},{4,20},{5,21},{6,22},{7,23},{8,24},{9,... | collective-permute-start | bytes 983048 | tf_op jit(solution)/shard_map/ppermute | solution.py:208
  20.4 9.0 %collective-permute-start.3 = (f32[4,40,512]{2,1,0:T(8,128)S(1)}, f32[4,40,512]{2,1,0:T(8,128)S(1)}, u32[]{:S(2)}, u32[]{:S(2)}) collective-permute-start(f32[4,40,512]{2,1,0:T(8,128)S(1)} %get-tuple-element.10), channel_id=1, source_target_pairs={{0,24},{1,25},{2,26},{3,27},{4,28},{5,29},{6,30},{7,31},{8,16},{9,... | collective-permute-start | bytes 983048 | tf_op jit(solution)/shard_map/ppermute | solution.py:208
  21.5 8.1 %collective-permute-start.2 = (f32[4,40,512]{2,1,0:T(8,128)S(1)}, f32[4,40,512]{2,1,0:T(8,128)S(1)}, u32[]{:S(2)}, u32[]{:S(2)}) collective-permute-start(f32[4,40,512]{2,1,0:T(8,128)S(1)} %get-tuple-element.11), channel_id=1, source_target_pairs={{0,8},{1,9},{2,10},{3,11},{4,12},{5,13},{6,14},{7,15},{8,0},{9,1},... | collective-permute-start | bytes 983048 | tf_op jit(solution)/shard_map/ppermute | solution.py:208

commit v2 on v1

v2 whole, which is shorter than its diff:
```python
import functools

import jax
import jax.numpy as jnp
from jax import lax
from jax.experimental import pallas as pl
from jax.experimental.pallas import tpu as pltpu
from jax.sharding import PartitionSpec as P

AXES = ("grp", "tile")
TORUS = 4
ROWS = 20
UNIT = 2 * ROWS
HALF = 512
VIRT = 256
NT = (((1,), (1,)), ((), ()))
ORDER = (2, 1, 3, 0)
SPLIT = (0, 3, 4)
FIRST = (0, 768, 2304, 4096, 5888, 7168, 7680)
OWN = (0, 7680)
DEPTH = 2


def coords(i):
    g, t = divmod(i, 32)
    z_lo, core = divmod(g, 2)
    x, r = divmod(t, 8)
    z_hi, y = divmod(r, 4)
    return x, y, z_hi * 2 + z_lo, core


def index(x, y, z, core):
    return ((z % 2) * 2 + core) * 32 + x * 8 + (z // 2) * 4 + y


def pairs(move):
    return [(i, index(*move(*coords(i)))) for i in range(128)]


OTHER_CORE = pairs(lambda x, y, z, c: (x, y, z, 1 - c))


def along_own(k):
    return pairs(lambda x, y, z, c: (x, y ^ k, z, c) if c else (x ^ k, y, z, c))


def plane_groups():
    groups = {}
    for i in range(128):
        x, y, z, c = coords(i)
        key, place = ((c, y), (x, z)) if c else ((c, x), (y, z))
        groups.setdefault(key, []).append((place, i))
    return [[i for _, i in sorted(g)] for g in groups.values()]


def mask_row(mask_ref, c0, width, occ):
    col = lax.broadcasted_iota(jnp.int32, (1, width), 1) + c0
    row = jnp.zeros((1, width), jnp.float32)
    for p in range(c0 // occ, (c0 + width - 1) // occ + 1):
        inside = (col >= p * occ) & (col < (p + 1) * occ)
        row = jnp.where(inside, mask_ref[p].astype(jnp.float32), row)
    return row.astype(jnp.bfloat16)


def here():
    g, t = lax.axis_index("grp"), lax.axis_index("tile")
    core, x, y = lax.rem(g, 2), t // 8, lax.rem(t, 4)
    return core, jnp.where(core == 0, x, y), jnp.where(core == 0, y, x)


def columns(bounds, k):
    return pl.ds(bounds[k], bounds[k + 1] - bounds[k])


def start_weights(w_ref, w_s, sem, side, cols):
    for z_lo in range(2):
        pltpu.make_async_copy(
            w_ref.at[z_lo, side, :, cols], w_s.at[pl.ds(z_lo * VIRT, VIRT), cols], sem
        ).start()


def wait_for(ref, sem):
    pltpu.make_async_copy(ref, ref, sem).wait()


def first_half(
    occ, owner_hbm, mask_hbm, amp_ref, w_ref, out_ref, x_ref, w_own,
    owner_ref, mask_ref, a_s, w_s, acc, a_sem, w_sem, own_sem, s_sem,
):
    core, own_at, other_at = here()
    blocks = len(FIRST) - 1
    rows = a_s.shape[0] // 32
    tables = [
        pltpu.make_async_copy(owner_hbm, owner_ref, s_sem.at[0]),
        pltpu.make_async_copy(mask_hbm, mask_ref, s_sem.at[1]),
    ]
    for table in tables:
        table.start()
    own_step, other_step = jnp.where(core == 0, 8, 1), jnp.where(core == 0, 1, 8)

    def start_amplitudes(k):
        for p, shift in enumerate(ORDER):
            for j in range(TORUS):
                for z_hi in range(2):
                    source = owner_ref[(own_at ^ shift) * own_step + j * other_step + z_hi * 4]
                    place = (p * TORUS + j) * 2 + z_hi
                    pltpu.make_async_copy(
                        amp_ref.at[pl.ds(source * rows, rows), :, columns(FIRST, k)],
                        a_s.at[pl.ds(place * rows, rows), :, columns(FIRST, k)],
                        a_sem.at[k],
                    ).start()

    for k in range(DEPTH):
        start_weights(w_ref, w_s, w_sem.at[k], 1 - core, columns(FIRST, k))
    for table in tables:
        table.wait()
    for k in range(DEPTH):
        start_amplitudes(k)
    for k in range(blocks):
        if k + DEPTH < blocks:
            start_weights(w_ref, w_s, w_sem.at[k + DEPTH], 1 - core, columns(FIRST, k + DEPTH))
            start_amplitudes(k + DEPTH)
        elif k < blocks - 1:
            n = k + DEPTH - blocks
            start_weights(w_ref, w_own, own_sem.at[n], core, columns(OWN, n))
        c0, c1 = FIRST[k], FIRST[k + 1]
        wait_for(a_s.at[:, :, columns(FIRST, k)], a_sem.at[k])
        amp = a_s[:, :, c0:c1].reshape(x_ref.shape[0], c1 - c0)
        x_ref[:, c0:c1] = amp * mask_row(mask_ref, c0, c1 - c0, occ)
        wait_for(w_s.at[:, columns(FIRST, k)], w_sem.at[k])
        part = lax.dot_general(x_ref[:, c0:c1], w_s[:, c0:c1], NT, preferred_element_type=jnp.float32)
        if k == 0:
            acc[...] = part
        elif k < blocks - 1:
            acc[...] += part
        else:
            total = acc[...] + part
            for p, shift in enumerate(ORDER):
                for j in range(TORUS):
                    u = p * TORUS + j
                    hop = j ^ other_at
                    at = jnp.where(hop == 0, 3, jnp.where(hop == 3, 2, jnp.where(hop == 2, 0, 1)))
                    out_ref[at, own_at ^ shift] = total[u * UNIT : (u + 1) * UNIT]
    for n in range(len(OWN) - 1):
        wait_for(w_own.at[:, columns(OWN, n)], own_sem.at[n])


def own_part(r0, r1, x_ref, w_ref, out_ref):
    part = lax.dot_general(x_ref[r0:r1], w_ref[...], NT, preferred_element_type=jnp.float32)
    out_ref[...] = part.reshape(out_ref.shape)


def shards(amplitudes, w_vvvo, pair_mask, owner_map):
    occ_total, roots, cols = amplitudes.shape
    rows = occ_total * roots
    w4 = w_vvvo.reshape(2, 2, VIRT, cols)
    any_spec = pl.BlockSpec(memory_space=pl.ANY)
    hbm = pl.BlockSpec(memory_space=pltpu.HBM)
    vmem = pl.BlockSpec(memory_space=pltpu.VMEM)

    def params(kib):
        return pltpu.CompilerParams(vmem_limit_bytes=kib * 1024)

    def cost(some_rows, moved):
        return pl.CostEstimate(flops=2 * some_rows * HALF * cols, bytes_accessed=moved, transcendentals=0)

    def part_shape(chunks):
        return pltpu.VMEM((chunks, TORUS, UNIT, HALF), jnp.float32)

    theirs, masked, weights = pl.pallas_call(
        functools.partial(first_half, cols // pair_mask.shape[0]),
        in_specs=[any_spec, any_spec, hbm, hbm],
        out_specs=[vmem, vmem, vmem],
        out_shape=[
            part_shape(TORUS),
            pltpu.VMEM((rows, cols), jnp.bfloat16),
            pltpu.VMEM((HALF, cols), jnp.bfloat16),
        ],
        scratch_shapes=[
            pltpu.SMEM(owner_map.shape, jnp.int32),
            pltpu.SMEM(pair_mask.shape, jnp.int32),
            pltpu.VMEM(amplitudes.shape, jnp.bfloat16),
            pltpu.VMEM((HALF, cols), jnp.bfloat16),
            pltpu.VMEM((rows, HALF), jnp.float32),
            pltpu.SemaphoreType.DMA((len(FIRST) - 1,)),
            pltpu.SemaphoreType.DMA((len(FIRST) - 1,)),
            pltpu.SemaphoreType.DMA((len(OWN) - 1,)),
            pltpu.SemaphoreType.DMA((2,)),
        ],
        compiler_params=params(43000),
        cost_estimate=cost(rows, 26 * 10**6),
        name="their_half",
    )(owner_map, pair_mask, amplitudes, w4)
    from_core = lax.ppermute(theirs, AXES, OTHER_CORE)
    chunk = rows // TORUS
    parts = []
    for n, (a, b) in enumerate(zip(SPLIT[:-1], SPLIT[1:])):
        parts.append(
            pl.pallas_call(
                functools.partial(own_part, a * chunk, b * chunk),
                in_specs=[vmem, vmem],
                out_specs=vmem,
                out_shape=part_shape(b - a),
                compiler_params=params(16000),
                cost_estimate=cost((b - a) * chunk, 0),
                name=f"own_part_{n}",
            )(masked, weights)
        )
    total = []
    for n, (a, b) in enumerate(zip(SPLIT[:-1], SPLIT[1:])):
        total += [parts[n][i - a] + from_core[i] for i in range(a, b)]
    arrived = [lax.ppermute(total[p], AXES, along_own(shift)) for p, shift in enumerate(ORDER) if shift]
    plane = total[-1] + arrived[0] + arrived[1] + arrived[2]
    sent = plane.reshape(TORUS, 2, ROWS, 2, VIRT).transpose(0, 1, 3, 2, 4).reshape(16, ROWS, VIRT)
    got = lax.all_to_all(sent, AXES, 0, 0, axis_index_groups=plane_groups(), tiled=True)
    return got.sum(axis=0).reshape(ROWS // roots, roots, VIRT)


def solution(mesh):
    return jax.shard_map(
        shards,
        mesh=mesh,
        in_specs=(P(None, None, AXES), P(None, AXES), P(AXES), P()),
        out_specs=P("tile", None, "grp"),
        check_vma=False,
    )
```

time: 47.8 us -> 44.2 us (0.925)
  waiting for transfers between devices: 8.06 us -> 5.37 us
  local copies, waits for them, and re-layouts: 2.24 us -> 0.86 us
  Pallas kernels: 15.4 us -> 16 us
    ppermute x3, waiting for transfers between devices: 8.05 us -> 5.37 us  [shards(): lax.ppermute(total[p], AXES, along_own(shift))]
    unnamed x4 -> x0, local copies, waits for them, and re-layouts: 1.31 us -> none
    pallas_call x1, Pallas kernels: 8.72 us -> 9.34 us  [shards(): pl.pallas_call(functools.partial(first_half, cols // pair_mask.shape[0]),...]
    pallas_call x1 -> x2, Pallas kernels: 6.67 us -> 6.66 us  [shards(): pl.pallas_call(functools.partial(own_part, a * chunk, b * chunk), in_spec...]
  transfers between devices with their start and end apart: 4 -> 4, of which waited for: 3 -> 3; matrix products, arithmetic and copies ran while one was open for 0% -> 0% of each run, Pallas kernels for 14% -> 15%
where the time goes in v2:
time: 44.2 us; the launch traced here: 44.1 us
  blocking collectives  17 us (38%)
  Pallas kernels  16 us (36%)
  waiting for transfers between devices  5.37 us (12%)
  starting transfers between devices  4.44 us (10%)
  local copies, waits for them, and re-layouts  0.86 us (2%)
    all_to_all x1, blocking collectives, shards(): lax.all_to_all(sent, AXES, 0, 0, axis_index_groups=plane_groups(), tiled=...  17 us
    pallas_call x1, Pallas kernels, shards(): pl.pallas_call(functools.partial(first_half, cols // pair_mask.shape[0]),...  9.34 us
    pallas_call x2, Pallas kernels, shards(): pl.pallas_call(functools.partial(own_part, a * chunk, b * chunk), in_spec...  6.66 us
    ppermute x3, waiting for transfers between devices, shards(): lax.ppermute(total[p], AXES, along_own(shift))  5.37 us
    ppermute x3, starting transfers between devices, shards(): lax.ppermute(total[p], AXES, along_own(shift))  4.36 us
  transfers between devices with their start and end apart: 4, of which 3 were waited for; matrix products, arithmetic and copies ran while one was open for 0% of the time, Pallas kernels for 15%

profile of v2, /device:TPU:0, one launch (start us, length us, event | category | flops | bytes accessed | tf_op | source)
XLA Modules:
  0.0 44.1 jit_solution(15098733656667479243)
XLA Ops:
  0.0 9.3 %their_half.1 = (f32[4,4,40,512]{3,2,1,0:T(8,128)S(1)}, bf16[640,7680]{1,0:T(8,128)(2,1)S(1)}, bf16[512,7680]{1,0:T(8,128)(2,1)S(1)}) custom-call(s32[32]{0:T(128)} %owner_hbm.1, s32[32]{0:T(128)} %mask_hbm.1, bf16[160,4,7680]{2,1,0:T(4,128)(2,1)} %amp_ref.1, bf16[2,2,256,7680]{3,2,1,0:T(8,128)(2,1)} %bitcast.18), custom_call_target="tpu_custom_call" | custom-call | flops 5033164800 | bytes 26000000 | tf_op jit(solution)/shard_map/their_half/pallas_call | solution.py:170
  9.3 0.1 collective-permute-start
  9.4 4.0 %own_part_0.1 = f32[3,4,40,512]{3,2,1,0:T(8,128)S(1)} custom-call(bf16[640,7680]{1,0:T(8,128)(2,1)S(1)} %get-tuple-element.8.x_ref, bf16[512,7680]{1,0:T(8,128)(2,1)S(1)} %get-tuple-element.9.w_ref), custom_call_target="tpu_custom_call" | custom-call | flops 3774873600 | tf_op jit(solution)/shard_map/own_part_0/pallas_call | solution.py:199
  13.4 0.0 collective-permute-done
  13.4 0.2 fusion.2
  13.6 3.2 %collective-permute-start.1 = (f32[4,40,512]{2,1,0:T(8,128)S(1)}, f32[4,40,512]{2,1,0:T(8,128)S(1)}, u32[]{:S(2)}, u32[]{:S(2)}) collective-permute-start(f32[4,40,512]{2,1,0:T(8,128)S(1)} %get-tuple-element.11), channel_id=1, source_target_pairs={{0,16},{1,17},{2,18},{3,19},{4,20},{5,21},{6,22},{7,23},{8,24},{9,... | collective-permute-start | bytes 983048 | tf_op jit(solution)/shard_map/ppermute | solution.py:212
  16.9 1.1 %collective-permute-start.3 = (f32[4,40,512]{2,1,0:T(8,128)S(1)}, f32[4,40,512]{2,1,0:T(8,128)S(1)}, u32[]{:S(2)}, u32[]{:S(2)}) collective-permute-start(f32[4,40,512]{2,1,0:T(8,128)S(1)} %get-tuple-element.12), channel_id=1, source_target_pairs={{0,24},{1,25},{2,26},{3,27},{4,28},{5,29},{6,30},{7,31},{8,16},{9,... | collective-permute-start | bytes 983048 | tf_op jit(solution)/shard_map/ppermute | solution.py:212
  18.0 0.0 collective-permute-start.2
  18.0 2.7 %own_part_1.1 = f32[1,4,40,512]{3,2,1,0:T(8,128)S(1)} custom-call(bf16[640,7680]{1,0:T(8,128)(2,1)S(1)} %get-tuple-element.8.x_ref, bf16[512,7680]{1,0:T(8,128)(2,1)S(1)} %get-tuple-element.9.w_ref), custom_call_target="tpu_custom_call" | custom-call | flops 1258291200 | tf_op jit(solution)/shard_map/own_part_1/pallas_call | solution.py:199
  20.7 1.7 %collective-permute-done.1 = f32[4,40,512]{2,1,0:T(8,128)S(1)} collective-permute-done((f32[4,40,512]{2,1,0:T(8,128)S(1)}, f32[4,40,512]{2,1,0:T(8,128)S(1)}, u32[]{:S(2)}, u32[]{:S(2)}) %collective-permute-start.1) | collective-permute-done | bytes 327712 | tf_op jit(solution)/shard_map/ppermute | solution.py:212
  22.4 3.4 %collective-permute-done.3 = f32[4,40,512]{2,1,0:T(8,128)S(1)} collective-permute-done((f32[4,40,512]{2,1,0:T(8,128)S(1)}, f32[4,40,512]{2,1,0:T(8,128)S(1)}, u32[]{:S(2)}, u32[]{:S(2)}) %collective-permute-start.3) | collective-permute-done | bytes 327712 | tf_op jit(solution)/shard_map/ppermute | solution.py:212
  25.8 0.2 collective-permute-done.2
  26.0 0.2 fusion.6
  26.2 0.2 reshape.17
  26.5 17.0 %all_to_all.5 = f32[16,20,256]{2,1,0:T(8,128)S(1)} all-to-all(f32[16,20,256]{2,1,0:T(8,128)S(1)} %bitcast.19), channel_id=1, replica_groups={{0,64,4,68,1,65,5,69,2,66,6,70,3,67,7,71},{8,72,12,76,9,73,13,77,10,74,..., dimensions={0} | all-to-all | bytes 655360 | tf_op jit(solution)/shard_map/all_to_all | solution.py:215
  43.5 0.6 %reshape.19 = f32[5,4,256]{2,1,0:T(4,128)} reshape(f32[20,256]{1,0:T(8,128)S(1)} %reduce_sum.9) | data formatting | bytes 40960 | tf_op jit(solution)/shard_map/reshape | solution.py:216
  (2 shorter events, 0.1 us)
Async XLA Ops:
  9.3 4.1 %collective-permute-start = (f32[4,4,40,512]{3,2,1,0:T(8,128)S(1)}, f32[4,4,40,512]{3,2,1,0:T(8,128)S(1)}, u32[]{:S(2)}, u32[]{:S(2)}) collective-permute-start(f32[4,4,40,512]{3,2,1,0:T(8,128)S(1)} %get-tuple-element.10), channel_id=1, source_target_pairs={{0,32},{1,33},{2,34},{3,35},{4,36},{5,37},{6,38},{7,39},{8,40},{9,... | collective-permute-start | bytes 3932168 | tf_op jit(solution)/shard_map/ppermute | solution.py:194
  13.6 8.7 %collective-permute-start.1 = (f32[4,40,512]{2,1,0:T(8,128)S(1)}, f32[4,40,512]{2,1,0:T(8,128)S(1)}, u32[]{:S(2)}, u32[]{:S(2)}) collective-permute-start(f32[4,40,512]{2,1,0:T(8,128)S(1)} %get-tuple-element.11), channel_id=1, source_target_pairs={{0,16},{1,17},{2,18},{3,19},{4,20},{5,21},{6,22},{7,23},{8,24},{9,... | collective-permute-start | bytes 983048 | tf_op jit(solution)/shard_map/ppermute | solution.py:212
  16.9 9.0 %collective-permute-start.3 = (f32[4,40,512]{2,1,0:T(8,128)S(1)}, f32[4,40,512]{2,1,0:T(8,128)S(1)}, u32[]{:S(2)}, u32[]{:S(2)}) collective-permute-start(f32[4,40,512]{2,1,0:T(8,128)S(1)} %get-tuple-element.12), channel_id=1, source_target_pairs={{0,24},{1,25},{2,26},{3,27},{4,28},{5,29},{6,30},{7,31},{8,16},{9,... | collective-permute-start | bytes 983048 | tf_op jit(solution)/shard_map/ppermute | solution.py:212
  18.0 8.1 %collective-permute-start.2 = (f32[4,40,512]{2,1,0:T(8,128)S(1)}, f32[4,40,512]{2,1,0:T(8,128)S(1)}, u32[]{:S(2)}, u32[]{:S(2)}) collective-permute-start(f32[4,40,512]{2,1,0:T(8,128)S(1)} %get-tuple-element.13), channel_id=1, source_target_pairs={{0,8},{1,9},{2,10},{3,11},{4,12},{5,13},{6,14},{7,15},{8,0},{9,1},... | collective-permute-start | bytes 983048 | tf_op jit(solution)/shard_map/ppermute | solution.py:212

commit v3 on v2

--- a/solution.py
+++ b/solution.py
@@ -14,8 +14,7 @@
 HALF = 512
 VIRT = 256
 NT = (((1,), (1,)), ((), ()))
-ORDER = (2, 1, 3, 0)
-SPLIT = (0, 3, 4)
+ORDER = (3, 1, 2, 0)
 FIRST = (0, 768, 2304, 4096, 5888, 7168, 7680)
 OWN = (0, 7680)
 DEPTH = 2
@@ -139,15 +138,31 @@
                 for j in range(TORUS):
                     u = p * TORUS + j
                     hop = j ^ other_at
-                    at = jnp.where(hop == 0, 3, jnp.where(hop == 3, 2, jnp.where(hop == 2, 0, 1)))
+                    at = sum(jnp.where(hop == h, n, 0) for n, h in enumerate(ORDER))
                     out_ref[at, own_at ^ shift] = total[u * UNIT : (u + 1) * UNIT]
     for n in range(len(OWN) - 1):
         wait_for(w_own.at[:, columns(OWN, n)], own_sem.at[n])
 
 
+def product(x_ref, r0, r1, c0, w_ref):
+    return lax.dot_general(
+        x_ref[r0:r1, c0 : c0 + w_ref.shape[1]], w_ref[...], NT, preferred_element_type=jnp.float32
+    )
+
+
 def own_part(r0, r1, x_ref, w_ref, out_ref):
-    part = lax.dot_general(x_ref[r0:r1], w_ref[...], NT, preferred_element_type=jnp.float32)
-    out_ref[...] = part.reshape(out_ref.shape)
+    out_ref[...] = product(x_ref, r0, r1, 0, w_ref).reshape(out_ref.shape)
+
+
+def plane_sum(kept_ref, core_ref, a_ref, b_ref, c_ref, out_ref):
+    for j in range(TORUS):
+        for z_hi in range(2):
+            rows = slice(z_hi * ROWS, (z_hi + 1) * ROWS)
+            total = kept_ref[0, j, rows] + core_ref[TORUS - 1, j, rows]
+            total = ((total + a_ref[j, rows]) + b_ref[j, rows]) + c_ref[j, rows]
+            for z_lo in range(2):
+                n = (j * 2 + z_hi) * 2 + z_lo
+                out_ref[n] = total[:, z_lo * VIRT : (z_lo + 1) * VIRT].reshape(out_ref.shape[1:])
 
 
 def shards(amplitudes, w_vvvo, pair_mask, owner_map):
@@ -174,7 +189,7 @@
         out_shape=[
             part_shape(TORUS),
             pltpu.VMEM((rows, cols), jnp.bfloat16),
-            pltpu.VMEM((HALF, cols), jnp.bfloat16),
+            pltpu.VMEM((HALF, OWN[-1]), jnp.bfloat16),
         ],
         scratch_shapes=[
             pltpu.SMEM(owner_map.shape, jnp.int32),
@@ -193,27 +208,36 @@
     )(owner_map, pair_mask, amplitudes, w4)
     from_core = lax.ppermute(theirs, AXES, OTHER_CORE)
     chunk = rows // TORUS
-    parts = []
-    for n, (a, b) in enumerate(zip(SPLIT[:-1], SPLIT[1:])):
-        parts.append(
-            pl.pallas_call(
-                functools.partial(own_part, a * chunk, b * chunk),
-                in_specs=[vmem, vmem],
-                out_specs=vmem,
-                out_shape=part_shape(b - a),
-                compiler_params=params(16000),
-                cost_estimate=cost((b - a) * chunk, 0),
-                name=f"own_part_{n}",
-            )(masked, weights)
-        )
-    total = []
-    for n, (a, b) in enumerate(zip(SPLIT[:-1], SPLIT[1:])):
-        total += [parts[n][i - a] + from_core[i] for i in range(a, b)]
-    arrived = [lax.ppermute(total[p], AXES, along_own(shift)) for p, shift in enumerate(ORDER) if shift]
-    plane = total[-1] + arrived[0] + arrived[1] + arrived[2]
-    sent = plane.reshape(TORUS, 2, ROWS, 2, VIRT).transpose(0, 1, 3, 2, 4).reshape(16, ROWS, VIRT)
+    sent_rows = (TORUS - 1) * chunk
+
+    def own(r0, r1, name):
+        return pl.pallas_call(
+            functools.partial(own_part, r0, r1),
+            in_specs=[vmem, vmem],
+            out_specs=vmem,
+            out_shape=part_shape((r1 - r0) // chunk),
+            compiler_params=params(16000),
+            cost_estimate=cost(r1 - r0, 0),
+            name=name,
+        )(masked, weights)
+
+    leaving = own(0, sent_rows, "own_sent")
+    kept = own(sent_rows, rows, "own_kept")
+    arrived = [
+        lax.ppermute(leaving[p] + from_core[p], AXES, along_own(shift))
+        for p, shift in enumerate(ORDER)
+        if shift
+    ]
+    sent = pl.pallas_call(
+        plane_sum,
+        in_specs=[vmem] * 5,
+        out_specs=vmem,
+        out_shape=pltpu.VMEM((16, ROWS // roots, roots, VIRT), jnp.float32),
+        compiler_params=params(16000),
+        name="plane_sum",
+    )(kept, from_core, *arrived)
     got = lax.all_to_all(sent, AXES, 0, 0, axis_index_groups=plane_groups(), tiled=True)
-    return got.sum(axis=0).reshape(ROWS // roots, roots, VIRT)
+    return got.sum(axis=0)
 
 
 def solution(mesh):

time: 44.2 us -> 43.6 us (0.986)
  local copies, waits for them, and re-layouts: 0.86 us -> 0 us
  other arithmetic: 0.38 us -> 0.86 us
    reshape x3 -> x0, local copies, waits for them, and re-layouts: 0.86 us -> none  [the longest x1 0.62 us: shards(): return got.sum(axis=0).reshape(ROWS // roots, roots, VIRT)]
    reduce_sum x1, other arithmetic: 0.03 us -> 0.67 us  [shards(): return got.sum(axis=0)]
    pallas_call x2 -> x3, Pallas kernels: 6.66 us -> 6.75 us  [the longest x2 6.66 us: own(): pl.pallas_call(functools.partial(own_part, r0, r1), in_specs=[vmem, vmem]...]
  transfers between devices with their start and end apart: 4 -> 4, of which waited for: 3 -> 2; matrix products, arithmetic and copies ran while one was open for 0% -> 0% of each run, Pallas kernels for 15% -> 15%
where the time goes in v3:
time: 43.6 us; the launch traced here: 43.5 us
  blocking collectives  16.7 us (38%)
  Pallas kernels  16.1 us (37%)
  waiting for transfers between devices  5.38 us (12%)
  starting transfers between devices  4.44 us (10%)
  other arithmetic  0.86 us (2%)
    all_to_all x1, blocking collectives, shards(): lax.all_to_all(sent, AXES, 0, 0, axis_index_groups=plane_groups(), tiled=...  16.7 us
    pallas_call x1, Pallas kernels, shards(): pl.pallas_call(functools.partial(first_half, cols // pair_mask.shape[0]),...  9.34 us
    pallas_call x2, Pallas kernels, own(): pl.pallas_call(functools.partial(own_part, r0, r1), in_specs=[vmem, vmem]...  6.66 us
    ppermute x3, waiting for transfers between devices, shards(): lax.ppermute(leaving[p] + from_core[p], AXES, along_own(shift))  5.38 us
    ppermute x3, starting transfers between devices, shards(): lax.ppermute(leaving[p] + from_core[p], AXES, along_own(shift))  4.36 us
  transfers between devices with their start and end apart: 4, of which 2 were waited for; matrix products, arithmetic and copies ran while one was open for 0% of the time, Pallas kernels for 15%

profile of v3, /device:TPU:0, one launch (start us, length us, event | category | flops | bytes accessed | tf_op | source)
XLA Modules:
  0.0 43.5 jit_solution(16938855022124214361)
XLA Ops:
  0.0 9.3 %their_half.1 = (f32[4,4,40,512]{3,2,1,0:T(8,128)S(1)}, bf16[640,7680]{1,0:T(8,128)(2,1)S(1)}, bf16[512,7680]{1,0:T(8,128)(2,1)S(1)}) custom-call(s32[32]{0:T(128)} %owner_hbm.1, s32[32]{0:T(128)} %mask_hbm.1, bf16[160,4,7680]{2,1,0:T(4,128)(2,1)} %amp_ref.1, bf16[2,2,256,7680]{3,2,1,0:T(8,128)(2,1)} %bitcast.7), custom_call_target="tpu_custom_call" | custom-call | flops 5033164800 | bytes 26000000 | tf_op jit(solution)/shard_map/their_half/pallas_call | solution.py:185
  9.3 0.1 collective-permute-start
  9.4 4.0 %own_sent.1 = f32[3,4,40,512]{3,2,1,0:T(8,128)S(1)} custom-call(bf16[640,7680]{1,0:T(8,128)(2,1)S(1)} %get-tuple-element.8.x_ref, bf16[512,7680]{1,0:T(8,128)(2,1)S(1)} %get-tuple-element.9.w_ref), custom_call_target="tpu_custom_call" | custom-call | flops 3774873600 | tf_op jit(solution)/shard_map/own_sent/pallas_call | solution.py:214
  13.4 0.0 collective-permute-done.core_ref
  13.4 0.2 fusion
  13.6 3.2 %collective-permute-start.3 = (f32[4,40,512]{2,1,0:T(8,128)S(1)}, f32[4,40,512]{2,1,0:T(8,128)S(1)}, u32[]{:S(2)}, u32[]{:S(2)}) collective-permute-start(f32[4,40,512]{2,1,0:T(8,128)S(1)} %get-tuple-element.11), channel_id=1, source_target_pairs={{0,16},{1,17},{2,18},{3,19},{4,20},{5,21},{6,22},{7,23},{8,24},{9,... | collective-permute-start | bytes 983048 | tf_op jit(solution)/shard_map/ppermute | solution.py:227
  16.9 0.6 %collective-permute-start.2 = (f32[4,40,512]{2,1,0:T(8,128)S(1)}, f32[4,40,512]{2,1,0:T(8,128)S(1)}, u32[]{:S(2)}, u32[]{:S(2)}) collective-permute-start(f32[4,40,512]{2,1,0:T(8,128)S(1)} %get-tuple-element.12), channel_id=1, source_target_pairs={{0,8},{1,9},{2,10},{3,11},{4,12},{5,13},{6,14},{7,15},{8,0},{9,1},... | collective-permute-start | bytes 983048 | tf_op jit(solution)/shard_map/ppermute | solution.py:227
  17.4 0.6 %collective-permute-start.1 = (f32[4,40,512]{2,1,0:T(8,128)S(1)}, f32[4,40,512]{2,1,0:T(8,128)S(1)}, u32[]{:S(2)}, u32[]{:S(2)}) collective-permute-start(f32[4,40,512]{2,1,0:T(8,128)S(1)} %get-tuple-element.13), channel_id=1, source_target_pairs={{0,24},{1,25},{2,26},{3,27},{4,28},{5,29},{6,30},{7,31},{8,16},{9,... | collective-permute-start | bytes 983048 | tf_op jit(solution)/shard_map/ppermute | solution.py:227
  18.0 2.7 %own_kept.1.kept_ref = f32[1,4,40,512]{3,2,1,0:T(8,128)S(1)} custom-call(bf16[640,7680]{1,0:T(8,128)(2,1)S(1)} %get-tuple-element.8.x_ref, bf16[512,7680]{1,0:T(8,128)(2,1)S(1)} %get-tuple-element.9.w_ref), custom_call_target="tpu_custom_call" | custom-call | flops 1258291200 | tf_op jit(solution)/shard_map/own_kept/pallas_call | solution.py:214
  20.7 1.6 %collective-permute-done.3.c_ref = f32[4,40,512]{2,1,0:T(8,128)S(1)} collective-permute-done((f32[4,40,512]{2,1,0:T(8,128)S(1)}, f32[4,40,512]{2,1,0:T(8,128)S(1)}, u32[]{:S(2)}, u32[]{:S(2)}) %collective-permute-start.3) | collective-permute-done | bytes 327712 | tf_op jit(solution)/shard_map/ppermute | solution.py:227
  22.3 3.7 %collective-permute-done.2.b_ref = f32[4,40,512]{2,1,0:T(8,128)S(1)} collective-permute-done((f32[4,40,512]{2,1,0:T(8,128)S(1)}, f32[4,40,512]{2,1,0:T(8,128)S(1)}, u32[]{:S(2)}, u32[]{:S(2)}) %collective-permute-start.2) | collective-permute-done | bytes 327712 | tf_op jit(solution)/shard_map/ppermute | solution.py:227
  26.0 0.0 collective-permute-done.1.a_ref
  26.0 0.1 plane_sum.1
  26.1 16.7 %all_to_all.5 = f32[16,5,4,256]{3,2,1,0:T(4,128)S(1)} all-to-all(f32[16,5,4,256]{3,2,1,0:T(4,128)S(1)} %plane_sum.1), channel_id=1, replica_groups={{0,64,4,68,1,65,5,69,2,66,6,70,3,67,7,71},{8,72,12,76,9,73,13,77,10,74,..., dimensions={0} | all-to-all | bytes 655360 | tf_op jit(solution)/shard_map/all_to_all | solution.py:239
  42.8 0.7 %reduce_sum.9 = f32[5,4,256]{2,1,0:T(4,128)} reduce(f32[16,5,4,256]{3,2,1,0:T(4,128)S(1)} %all_to_all.5, f32[]{:T(128)} %constant.0.clone.1), dimensions={0}, to_apply=%region_0.0 | reduce | flops 76800 | bytes 348164 | tf_op jit(solution)/shard_map/reduce_sum | solution.py:240
Async XLA Ops:
  9.3 4.1 %collective-permute-start = (f32[4,4,40,512]{3,2,1,0:T(8,128)S(1)}, f32[4,4,40,512]{3,2,1,0:T(8,128)S(1)}, u32[]{:S(2)}, u32[]{:S(2)}) collective-permute-start(f32[4,4,40,512]{3,2,1,0:T(8,128)S(1)} %get-tuple-element.10), channel_id=1, source_target_pairs={{0,32},{1,33},{2,34},{3,35},{4,36},{5,37},{6,38},{7,39},{8,40},{9,... | collective-permute-start | bytes 3932168 | tf_op jit(solution)/shard_map/ppermute | solution.py:209
  13.6 8.7 %collective-permute-start.3 = (f32[4,40,512]{2,1,0:T(8,128)S(1)}, f32[4,40,512]{2,1,0:T(8,128)S(1)}, u32[]{:S(2)}, u32[]{:S(2)}) collective-permute-start(f32[4,40,512]{2,1,0:T(8,128)S(1)} %get-tuple-element.11), channel_id=1, source_target_pairs={{0,16},{1,17},{2,18},{3,19},{4,20},{5,21},{6,22},{7,23},{8,24},{9,... | collective-permute-start | bytes 983048 | tf_op jit(solution)/shard_map/ppermute | solution.py:227
  16.9 9.2 %collective-permute-start.2 = (f32[4,40,512]{2,1,0:T(8,128)S(1)}, f32[4,40,512]{2,1,0:T(8,128)S(1)}, u32[]{:S(2)}, u32[]{:S(2)}) collective-permute-start(f32[4,40,512]{2,1,0:T(8,128)S(1)} %get-tuple-element.12), channel_id=1, source_target_pairs={{0,8},{1,9},{2,10},{3,11},{4,12},{5,13},{6,14},{7,15},{8,0},{9,1},... | collective-permute-start | bytes 983048 | tf_op jit(solution)/shard_map/ppermute | solution.py:227
  17.4 8.6 %collective-permute-start.1 = (f32[4,40,512]{2,1,0:T(8,128)S(1)}, f32[4,40,512]{2,1,0:T(8,128)S(1)}, u32[]{:S(2)}, u32[]{:S(2)}) collective-permute-start(f32[4,40,512]{2,1,0:T(8,128)S(1)} %get-tuple-element.13), channel_id=1, source_target_pairs={{0,24},{1,25},{2,26},{3,27},{4,28},{5,29},{6,30},{7,31},{8,16},{9,... | collective-permute-start | bytes 983048 | tf_op jit(solution)/shard_map/ppermute | solution.py:227

commit v4 on v3

--- a/solution.py
+++ b/solution.py
@@ -16,7 +16,7 @@
 NT = (((1,), (1,)), ((), ()))
 ORDER = (3, 1, 2, 0)
 FIRST = (0, 768, 2304, 4096, 5888, 7168, 7680)
-OWN = (0, 7680)
+OWN = (0, 2560, 5120, 7680)
 DEPTH = 2
 
 
@@ -119,8 +119,8 @@
         if k + DEPTH < blocks:
             start_weights(w_ref, w_s, w_sem.at[k + DEPTH], 1 - core, columns(FIRST, k + DEPTH))
             start_amplitudes(k + DEPTH)
-        elif k < blocks - 1:
-            n = k + DEPTH - blocks
+        n = k + len(OWN) - blocks
+        if 0 <= n < len(OWN) - 1:
             start_weights(w_ref, w_own, own_sem.at[n], core, columns(OWN, n))
         c0, c1 = FIRST[k], FIRST[k + 1]
         wait_for(a_s.at[:, :, columns(FIRST, k)], a_sem.at[k])

time: 43.6 us -> 43.2 us (level)
  no operation moved by 1% of the time
where the time goes in v4:
time: 43.2 us; the launch traced here: 43.1 us
  blocking collectives  16.7 us (39%)
  Pallas kernels  15.7 us (36%)
  waiting for transfers between devices  5.38 us (12%)
  starting transfers between devices  4.44 us (10%)
  other arithmetic  0.86 us (2%)
    all_to_all x1, blocking collectives, shards(): lax.all_to_all(sent, AXES, 0, 0, axis_index_groups=plane_groups(), tiled=...  16.7 us
    pallas_call x1, Pallas kernels, shards(): pl.pallas_call(functools.partial(first_half, cols // pair_mask.shape[0]),...  8.94 us
    pallas_call x2, Pallas kernels, own(): pl.pallas_call(functools.partial(own_part, r0, r1), in_specs=[vmem, vmem]...  6.66 us
    ppermute x3, waiting for transfers between devices, shards(): lax.ppermute(leaving[p] + from_core[p], AXES, along_own(shift))  5.38 us
    ppermute x3, starting transfers between devices, shards(): lax.ppermute(leaving[p] + from_core[p], AXES, along_own(shift))  4.35 us
  transfers between devices with their start and end apart: 4, of which 2 were waited for; matrix products, arithmetic and copies ran while one was open for 0% of the time, Pallas kernels for 15%

profile of v4, /device:TPU:0, one launch (start us, length us, event | category | flops | bytes accessed | tf_op | source)
XLA Modules:
  0.0 43.1 jit_solution(8933685498035874557)
XLA Ops:
  0.0 8.9 %their_half.1 = (f32[4,4,40,512]{3,2,1,0:T(8,128)S(1)}, bf16[640,7680]{1,0:T(8,128)(2,1)S(1)}, bf16[512,7680]{1,0:T(8,128)(2,1)S(1)}) custom-call(s32[32]{0:T(128)} %owner_hbm.1, s32[32]{0:T(128)} %mask_hbm.1, bf16[160,4,7680]{2,1,0:T(4,128)(2,1)} %amp_ref.1, bf16[2,2,256,7680]{3,2,1,0:T(8,128)(2,1)} %bitcast.7), custom_call_target="tpu_custom_call" | custom-call | flops 5033164800 | bytes 26000000 | tf_op jit(solution)/shard_map/their_half/pallas_call | solution.py:185
  8.9 0.1 collective-permute-start
  9.0 4.0 %own_sent.1 = f32[3,4,40,512]{3,2,1,0:T(8,128)S(1)} custom-call(bf16[640,7680]{1,0:T(8,128)(2,1)S(1)} %get-tuple-element.8.x_ref, bf16[512,7680]{1,0:T(8,128)(2,1)S(1)} %get-tuple-element.9.w_ref), custom_call_target="tpu_custom_call" | custom-call | flops 3774873600 | tf_op jit(solution)/shard_map/own_sent/pallas_call | solution.py:214
  13.0 0.0 collective-permute-done.core_ref
  13.0 0.2 fusion
  13.2 3.2 %collective-permute-start.3 = (f32[4,40,512]{2,1,0:T(8,128)S(1)}, f32[4,40,512]{2,1,0:T(8,128)S(1)}, u32[]{:S(2)}, u32[]{:S(2)}) collective-permute-start(f32[4,40,512]{2,1,0:T(8,128)S(1)} %get-tuple-element.11), channel_id=1, source_target_pairs={{0,16},{1,17},{2,18},{3,19},{4,20},{5,21},{6,22},{7,23},{8,24},{9,... | collective-permute-start | bytes 983048 | tf_op jit(solution)/shard_map/ppermute | solution.py:227
  16.5 0.6 %collective-permute-start.2 = (f32[4,40,512]{2,1,0:T(8,128)S(1)}, f32[4,40,512]{2,1,0:T(8,128)S(1)}, u32[]{:S(2)}, u32[]{:S(2)}) collective-permute-start(f32[4,40,512]{2,1,0:T(8,128)S(1)} %get-tuple-element.12), channel_id=1, source_target_pairs={{0,8},{1,9},{2,10},{3,11},{4,12},{5,13},{6,14},{7,15},{8,0},{9,1},... | collective-permute-start | bytes 983048 | tf_op jit(solution)/shard_map/ppermute | solution.py:227
  17.0 0.6 %collective-permute-start.1 = (f32[4,40,512]{2,1,0:T(8,128)S(1)}, f32[4,40,512]{2,1,0:T(8,128)S(1)}, u32[]{:S(2)}, u32[]{:S(2)}) collective-permute-start(f32[4,40,512]{2,1,0:T(8,128)S(1)} %get-tuple-element.13), channel_id=1, source_target_pairs={{0,24},{1,25},{2,26},{3,27},{4,28},{5,29},{6,30},{7,31},{8,16},{9,... | collective-permute-start | bytes 983048 | tf_op jit(solution)/shard_map/ppermute | solution.py:227
  17.6 2.7 %own_kept.1.kept_ref = f32[1,4,40,512]{3,2,1,0:T(8,128)S(1)} custom-call(bf16[640,7680]{1,0:T(8,128)(2,1)S(1)} %get-tuple-element.8.x_ref, bf16[512,7680]{1,0:T(8,128)(2,1)S(1)} %get-tuple-element.9.w_ref), custom_call_target="tpu_custom_call" | custom-call | flops 1258291200 | tf_op jit(solution)/shard_map/own_kept/pallas_call | solution.py:214
  20.3 1.6 %collective-permute-done.3.c_ref = f32[4,40,512]{2,1,0:T(8,128)S(1)} collective-permute-done((f32[4,40,512]{2,1,0:T(8,128)S(1)}, f32[4,40,512]{2,1,0:T(8,128)S(1)}, u32[]{:S(2)}, u32[]{:S(2)}) %collective-permute-start.3) | collective-permute-done | bytes 327712 | tf_op jit(solution)/shard_map/ppermute | solution.py:227
  21.9 3.7 %collective-permute-done.2.b_ref = f32[4,40,512]{2,1,0:T(8,128)S(1)} collective-permute-done((f32[4,40,512]{2,1,0:T(8,128)S(1)}, f32[4,40,512]{2,1,0:T(8,128)S(1)}, u32[]{:S(2)}, u32[]{:S(2)}) %collective-permute-start.2) | collective-permute-done | bytes 327712 | tf_op jit(solution)/shard_map/ppermute | solution.py:227
  25.7 0.0 collective-permute-done.1.a_ref
  25.7 0.1 plane_sum.1
  25.8 16.7 %all_to_all.5 = f32[16,5,4,256]{3,2,1,0:T(4,128)S(1)} all-to-all(f32[16,5,4,256]{3,2,1,0:T(4,128)S(1)} %plane_sum.1), channel_id=1, replica_groups={{0,64,4,68,1,65,5,69,2,66,6,70,3,67,7,71},{8,72,12,76,9,73,13,77,10,74,..., dimensions={0} | all-to-all | bytes 655360 | tf_op jit(solution)/shard_map/all_to_all | solution.py:239
  42.4 0.7 %reduce_sum.9 = f32[5,4,256]{2,1,0:T(4,128)} reduce(f32[16,5,4,256]{3,2,1,0:T(4,128)S(1)} %all_to_all.5, f32[]{:T(128)} %constant.0.clone.1), dimensions={0}, to_apply=%region_0.0 | reduce | flops 76800 | bytes 348164 | tf_op jit(solution)/shard_map/reduce_sum | solution.py:240
Async XLA Ops:
  8.9 4.1 %collective-permute-start = (f32[4,4,40,512]{3,2,1,0:T(8,128)S(1)}, f32[4,4,40,512]{3,2,1,0:T(8,128)S(1)}, u32[]{:S(2)}, u32[]{:S(2)}) collective-permute-start(f32[4,4,40,512]{3,2,1,0:T(8,128)S(1)} %get-tuple-element.10), channel_id=1, source_target_pairs={{0,32},{1,33},{2,34},{3,35},{4,36},{5,37},{6,38},{7,39},{8,40},{9,... | collective-permute-start | bytes 3932168 | tf_op jit(solution)/shard_map/ppermute | solution.py:209
  13.2 8.7 %collective-permute-start.3 = (f32[4,40,512]{2,1,0:T(8,128)S(1)}, f32[4,40,512]{2,1,0:T(8,128)S(1)}, u32[]{:S(2)}, u32[]{:S(2)}) collective-permute-start(f32[4,40,512]{2,1,0:T(8,128)S(1)} %get-tuple-element.11), channel_id=1, source_target_pairs={{0,16},{1,17},{2,18},{3,19},{4,20},{5,21},{6,22},{7,23},{8,24},{9,... | collective-permute-start | bytes 983048 | tf_op jit(solution)/shard_map/ppermute | solution.py:227
  16.5 9.2 %collective-permute-start.2 = (f32[4,40,512]{2,1,0:T(8,128)S(1)}, f32[4,40,512]{2,1,0:T(8,128)S(1)}, u32[]{:S(2)}, u32[]{:S(2)}) collective-permute-start(f32[4,40,512]{2,1,0:T(8,128)S(1)} %get-tuple-element.12), channel_id=1, source_target_pairs={{0,8},{1,9},{2,10},{3,11},{4,12},{5,13},{6,14},{7,15},{8,0},{9,1},... | collective-permute-start | bytes 983048 | tf_op jit(solution)/shard_map/ppermute | solution.py:227
  17.0 8.6 %collective-permute-start.1 = (f32[4,40,512]{2,1,0:T(8,128)S(1)}, f32[4,40,512]{2,1,0:T(8,128)S(1)}, u32[]{:S(2)}, u32[]{:S(2)}) collective-permute-start(f32[4,40,512]{2,1,0:T(8,128)S(1)} %get-tuple-element.13), channel_id=1, source_target_pairs={{0,24},{1,25},{2,26},{3,27},{4,28},{5,29},{6,30},{7,31},{8,16},{9,... | collective-permute-start | bytes 983048 | tf_op jit(solution)/shard_map/ppermute | solution.py:227
